TPU v7x, 128 devices: a whole 4x4x4 slice. The times are simulated.
128 devices in a mesh: fsdp: 8 (over x_lo, y), seq: 16 (over x_hi, z, core).
Axes of the slice: x: 4 (x_hi: 2, x_lo: 2; x = x_hi * 2 + x_lo), y: 4, z: 4, core: 2. Of those that a mesh axis runs over, the one named last changes fastest.
Arguments:
- image_input: bfloat16 [8, 2048, 1536], P('fsdp', 'seq'), may hold values from -6 to 6
- text_input: bfloat16 [8, 128, 1536], P('fsdp'), may hold values from -6 to 6
- w_qkv: bfloat16 [1536, 3, 2048], P('fsdp'), may hold values from -0.15625 to 0.15625
- query_gain: float32 [128], replicated, may hold values from 1.2 to 2.4
- key_gain: float32 [128], replicated, may hold values from 1.2 to 2.4
- image_cotangent: bfloat16 [8, 2048, 2048], P('fsdp', 'seq'), may hold values from -6 to 6
- text_cotangent: bfloat16 [8, 128, 2048], P('fsdp'), may hold values from -6 to 6
Outputs:
- image_grad: bfloat16 [8, 2048, 1536], P('fsdp', 'seq')
- text_grad: bfloat16 [8, 128, 1536], P('fsdp')
- weight_grad: float32 [1536, 3, 2048], P('fsdp', None, 'seq')
- gain_grad: float32 [2, 128], replicated
All inputs are finite; a program needn't handle non-finite values.
Results may differ from a plain program's by a relative error of at most 0.018.
The roundings to bfloat16 on the way count: a program that leaves them out, or rounds other values in their place, can miss the bound.
Values may be sent and summed in bfloat16 or wider, within the bound.
A program may use at most 192 MiB of HBM per device.

v0:
```python
import math
import jax
import jax.numpy as jnp
from jax import lax
from jax.sharding import Mesh
from jax.sharding import PartitionSpec as P

HEADS = 16
HEAD = 128
SEQ = ("seq_0", "seq_1", "seq_2")
FSDP = ("fsdp_0", "fsdp_1")
FSDP_SEQ = ("fsdp_0", "fsdp_1", "seq_0", "seq_1", "seq_2")
epsilon = 1e-06
query_parts = 4


def over_axes(shard, axes):
    for axis in axes:
        shard = lax.psum(shard, axis)
    return shard


def sent_to_all(shard, axis):
    copies = jnp.broadcast_to(shard, (lax.axis_size(axis), *shard.shape))
    return lax.all_to_all(copies, axis, split_axis=0, concat_axis=0, tiled=True)


def in_order(pieces, dim):
    pieces = jnp.moveaxis(pieces, 0, dim)
    lengths = pieces.shape
    return pieces.reshape(*lengths[:dim], lengths[dim] * lengths[dim + 1], *lengths[dim + 2 :])


def collect(shard, axis, dim):
    pieces = sent_to_all(shard, axis)
    return in_order(pieces, dim)


def rms_forward(values, gain):
    floated = values.astype(jnp.float32)
    inverse = lax.rsqrt(jnp.mean(floated * floated, axis=-1, keepdims=True) + epsilon)
    return (floated, inverse, (floated * inverse * gain).astype(jnp.bfloat16))


def rms_backward(floated, inverse, gain, incoming):
    weighted = incoming * gain
    inner_mean = jnp.mean(weighted * floated, axis=-1, keepdims=True)
    grad_input = inverse * weighted - floated * inverse * inverse * inverse * inner_mean
    grad_gain = jnp.sum(incoming * floated * inverse, axis=0)
    return (grad_input, grad_gain)


def head_backward(query_rows, key_rows, value_rows, incoming, query_gain, key_gain):
    query_float, query_inverse, query_normed = rms_forward(query_rows, query_gain)
    key_float, key_inverse, key_normed = rms_forward(key_rows, key_gain)
    length = query_rows.shape[0]
    width = query_rows.shape[1]
    block_rows = length // query_parts
    factor = 1.0 / math.sqrt(width)
    query_blocks = query_normed.reshape(query_parts, block_rows, width)
    incoming_blocks = incoming.reshape(query_parts, block_rows, width)

    def visit(carried, pieces):
        key_total, value_total = carried
        query_piece, incoming_piece = pieces
        scores = jnp.dot(query_piece, key_normed.T, preferred_element_type=jnp.float32) * factor
        attention = jax.nn.softmax(scores, axis=-1)
        attention_grad = jnp.dot(incoming_piece, value_rows.T, preferred_element_type=jnp.float32)
        row_dot = jnp.sum(attention * attention_grad, axis=-1, keepdims=True)
        score_grad = (attention * (attention_grad - row_dot)).astype(jnp.bfloat16)
        value_total = value_total + jnp.dot(
            attention.astype(jnp.bfloat16).T, incoming_piece, preferred_element_type=jnp.float32
        )
        key_total = (
            key_total
            + jnp.dot(score_grad.T, query_piece, preferred_element_type=jnp.float32) * factor
        )
        query_grad = jnp.dot(score_grad, key_normed, preferred_element_type=jnp.float32) * factor
        return ((key_total, value_total), query_grad)

    zeros_init = jnp.zeros((length, width), jnp.float32)
    (key_total, value_total), query_pieces = lax.scan(
        visit, (zeros_init, zeros_init), (query_blocks, incoming_blocks)
    )
    query_grad = query_pieces.reshape(length, width)
    query_input_grad, query_gain_grad = rms_backward(
        query_float, query_inverse, query_gain, query_grad
    )
    key_input_grad, key_gain_grad = rms_backward(key_float, key_inverse, key_gain, key_total)
    stacked = jnp.stack([query_input_grad, key_input_grad, value_total], axis=1).astype(
        jnp.bfloat16
    )
    return (stacked, jnp.stack([query_gain_grad, key_gain_grad], axis=0))


def local(image_input, text_input, w_qkv, query_gain, key_gain, image_cotangent, text_cotangent):
    member_count = lax.axis_size(SEQ)
    own_index = lax.axis_index(SEQ)
    local_heads = HEADS // member_count
    own_width = local_heads * HEAD
    offset = own_index * own_width
    text_length = text_input.shape[1]
    image_rows_dev = image_input.shape[1]
    weights = lax.all_gather(w_qkv, FSDP, axis=0, tiled=True)
    image_triple = jnp.einsum(
        "btd,dch->btch", image_input, weights, preferred_element_type=jnp.float32
    ).astype(jnp.bfloat16)
    stacked = jnp.concatenate([image_triple, image_cotangent[:, :, None, :]], axis=2)
    arrived = lax.all_to_all(stacked, SEQ, split_axis=3, concat_axis=1, tiled=True)
    own_weights = lax.dynamic_slice_in_dim(weights, offset, own_width, 2)
    text_triple = jnp.einsum(
        "btd,dch->btch", text_input, own_weights, preferred_element_type=jnp.float32
    ).astype(jnp.bfloat16)
    text_incoming = lax.dynamic_slice_in_dim(text_cotangent, offset, own_width, 2)
    joined_triple = jnp.concatenate([text_triple, arrived[:, :, :3]], axis=1)
    joined_incoming = jnp.concatenate([text_incoming, arrived[:, :, 3]], axis=1)
    batch_rows = joined_triple.shape[0]
    length = joined_triple.shape[1]
    split_triple = joined_triple.reshape(batch_rows, length, 3, local_heads, HEAD)
    split_incoming = joined_incoming.reshape(batch_rows, length, local_heads, HEAD)
    per_head = jax.vmap(head_backward, in_axes=(1, 1, 1, 1, None, None), out_axes=(2, 0))
    per_batch = jax.vmap(per_head, in_axes=(0, 0, 0, 0, None, None), out_axes=(0, 0))
    head_grads, gain_parts = per_batch(
        split_triple[:, :, 0],
        split_triple[:, :, 1],
        split_triple[:, :, 2],
        split_incoming,
        query_gain,
        key_gain,
    )
    head_grads = head_grads.reshape(batch_rows, length, 3, own_width)
    text_grads = head_grads[:, :text_length]
    image_grads = head_grads[:, text_length:]
    gain_total = over_axes(jnp.sum(gain_parts, axis=(0, 1)), FSDP_SEQ)
    image_tokens, text_share = (
        lax.all_to_all(image_grads, SEQ, split_axis=1, concat_axis=3, tiled=True),
        lax.all_to_all(text_grads, SEQ, split_axis=1, concat_axis=3, tiled=True),
    )
    text_piece = jnp.einsum(
        "btch,dch->btd", text_share, weights, preferred_element_type=jnp.float32
    ).astype(jnp.bfloat16)
    text_out = collect(text_piece, SEQ, 1)
    image_out = jnp.einsum(
        "btch,dch->btd", image_tokens, weights, preferred_element_type=jnp.float32
    ).astype(jnp.bfloat16)
    text_part = jnp.einsum(
        "btd,btch->dch", text_input, text_grads, preferred_element_type=jnp.float32
    )
    whole_image = lax.all_gather(image_input, SEQ, axis=1, tiled=True)

    def add_block(block, running):
        start = (block * image_rows_dev).astype(jnp.int32)
        image_block = lax.dynamic_slice_in_dim(whole_image, start, image_rows_dev, 1)
        grad_block = lax.dynamic_slice_in_dim(image_grads, start, image_rows_dev, 1)
        selected = (block == own_index).astype(jnp.float32)
        term = (
            jnp.einsum("btd,btch->dch", image_block, grad_block, preferred_element_type=jnp.float32)
            + text_part * selected
        )
        rounded = lax.optimization_barrier(term.astype(jnp.bfloat16))
        return running + rounded.astype(jnp.float32)

    start_total = jnp.zeros((image_input.shape[2], 3, own_width), jnp.float32)
    head_total = lax.fori_loop(0, member_count, add_block, start_total)
    grad_weights = lax.psum_scatter(
        head_total.astype(jnp.bfloat16), FSDP, scatter_dimension=0, tiled=True
    ).astype(jnp.float32)
    return (image_out, text_out, grad_weights, gain_total)


def solution(mesh):
    finer = Mesh(
        mesh.devices.reshape(2, 4, 2, 4, 2), ("fsdp_0", "fsdp_1", "seq_0", "seq_1", "seq_2")
    )
    return jax.shard_map(
        local,
        mesh=finer,
        in_specs=(
            P(FSDP, SEQ, None),
            P(FSDP, None, None),
            P(FSDP, None, None),
            P(),
            P(),
            P(FSDP, SEQ, None),
            P(FSDP, None, None),
        ),
        out_specs=(P(FSDP, SEQ, None), P(FSDP, None, None), P(FSDP, None, SEQ), P()),
        check_vma=False,
    )
```

profile of v0, /device:TPU:1, one launch (start us, length us, event | category | flops | bytes accessed | tf_op | source)
XLA Modules:
  0.0 568.3 jit_solution(10059944847568096801)
XLA Ops:
  8.8 194.9 %all-gather.3.cloned.1.call-done = bf16[1536,3,2048]{2,0,1:T(8,128)(2,1)} async-done(((bf16[192,3,2048]{2,0,1:T(8,128)(2,1)}), bf16[1536,3,2048]{2,0,1:T(8,128)(2,1)}) %all-gather.3.cloned.1.call-update) | async-done | bytes 18874384 | tf_op jit(solution)/shard_map/all_gather | solution.py:104
  203.7 9.0 %fusion.31 = bf16[1,128,3,2048]{3,1,2,0:T(8,128)(2,1)S(1)} fusion(bf16[1536,3,2048]{2,0,1:T(8,128)(2,1)} %all-gather.3.cloned.1.call-done, bf16[1,128,1536]{2,1,0:T(8,128)(2,1)S(1)} %copy-done.15), kind=kOutput, calls=%fused_computation.41 | convolution fusion | flops 2416705536 | bytes 20840448 | tf_op jit(solution)/shard_map/btd,dch->btch/dot_general | solution.py:105
  215.5 7.4 %all-to-all-start = ((bf16[1,128,4,2048]{1,2,0,3:T(4,128)(2,1)}), bf16[1,128,4,2048]{1,2,0,3:T(4,128)(2,1)}, u32[]{:S(2)}, u32[]{:S(2)}) async-start(bf16[1,128,4,2048]{1,2,0,3:T(4,128)(2,1)} %copy.49), calls=%async_computation | async-start | bytes 4194304 | tf_op jit(solution)/shard_map/all_to_all | solution.py:109
  225.9 29.6 %all-to-all-done = bf16[1,128,4,2048]{1,2,0,3:T(4,128)(2,1)} async-done(((bf16[1,128,4,2048]{1,2,0,3:T(4,128)(2,1)}), bf16[1,128,4,2048]{1,2,0,3:T(4,128)(2,1)}, u32[]{:S(2)}, u32[]{:S(2)}) %all-to-all-start) | async-done | bytes 2097184 | tf_op jit(solution)/shard_map/all_to_all | solution.py:109
  255.5 4.3 copy.80
  259.8 4.2 all_to_all.41
  281.7 71.7 %while.29 = (s32[]{:T(128)}, f32[1,1,2176,128]{3,2,1,0:T(8,128)S(1)}, f32[1,1,2176,128]{3,2,1,0:T(8,128)}, f32[4,1,1,544,128]{4,3,2,1,0:T(8,128)}, bf16[4,1,1,54...) while((s32[]{:T(128)}, ...), condition=%wide.region_6.7_spmd.clone, body=%wide.region_2.6_spmd.clone.sunk | while | flops 1535592832 | bytes 89573472 | solution.py:82
  286.7 4.8 fusion.106
  304.3 5.1 fusion.106
  322.4 5.2 fusion.106
  340.4 5.1 fusion.106
  369.6 7.2 %all-to-all-start.2 = ((bf16[1,128,3,128]{3,2,0,1:T(4,128)(2,1)}), bf16[1,128,3,128]{3,2,0,1:T(4,128)(2,1)S(1)}, u32[]{:S(2)}, u32[]{:S(2)}) async-start(bf16[1,128,3,128]{3,2,0,1:T(4,128)(2,1)} %copy.65), calls=%async_computation.2 | async-start | bytes 262144 | tf_op jit(solution)/shard_map/all_to_all | solution.py:137
  379.3 5.1 all-to-all-done.2
  384.4 9.0 %fusion.34 = bf16[8,1536]{1,0:T(8,128)(2,1)S(1)} fusion(bf16[1536,3,2048]{2,0,1:T(8,128)(2,1)} %all-gather.3.cloned.1.call-done, bf16[1,128,3,128]{3,2,0,1:T(4,128)(2,1)S(1)} %all-to-all-done.2), kind=kOutput, calls=%fused_computation.46 | convolution fusion | flops 151007232 | bytes 18997248 | tf_op jit(solution)/shard_map/btch,dch->btd/dot_general | solution.py:139
  394.2 4.0 all-to-all-start.3
  401.1 6.9 %all-to-all-done.3 = bf16[16,1,8,1536]{3,2,1,0:T(8,128)(2,1)S(1)} async-done(((bf16[16,1,8,1536]{3,2,1,0:T(8,128)(2,1)}), bf16[16,1,8,1536]{3,2,1,0:T(8,128)(2,1)S(1)}, u32[]{:S(2)}, u32[]{:S(2)}) %all-to-all-start.3) | async-done | bytes 393248 | tf_op jit(solution)/shard_map/all_to_all | solution.py:25
  408.8 5.4 all-to-all-start.1
  414.3 87.6 %while.30 = (s32[]{:T(128)}, f32[1536,3,128]{2,0,1:T(8,128)}, bf16[1,2048,1536]{1,2,0:T(8,128)(2,1)}, bf16[1,2048,3,128]{1,3,2,0:T(8,128)(2,1)S(1)}, s32[]{:T(12...) while((s32[]{:T(128)}, f32[1536,3,128]{2,0,1:T(8,128)}, ...), condition=%wide.region_10.11_spmd.clone, body=%wide.region_9.10_spmd.clone.sunk | while | flops 154533888 | bytes 9930411 | solution.py:164
  508.6 6.1 %psum.36 = f32[2,128]{1,0:T(2,128)S(1)} all-reduce(f32[2,128]{1,0:T(2,128)S(1)} %psum.35), channel_id=1, replica_groups=mesh['fsdp_0'=2,'fsdp_1'=4,'seq_0'=2,'seq_1'=4,'seq_2'=2] {'fsdp_1'}, use_global_device_ids=true, to_apply=%region_15.16 | all-reduce | flops 256 | bytes 2048 | tf_op jit(solution)/shard_map/psum | solution.py:19
  514.7 5.7 psum.37
  520.4 9.2 %psum.38 = f32[2,128]{1,0:T(2,128)S(1)} all-reduce(f32[2,128]{1,0:T(2,128)S(1)} %psum.37), channel_id=1, replica_groups=mesh['fsdp_0'=2,'fsdp_1'=4,'seq_0'=2,'seq_1'=4,'seq_2'=2] {'seq_1'}, use_global_device_ids=true, to_apply=%region_17.18 | all-reduce | flops 256 | bytes 2048 | tf_op jit(solution)/shard_map/psum | solution.py:19
  529.6 8.8 %psum.39 = f32[2,128]{1,0:T(2,128)} all-reduce(f32[2,128]{1,0:T(2,128)S(1)} %psum.38), channel_id=1, replica_groups=mesh['fsdp_0'=2,'fsdp_1'=4,'seq_0'=2,'seq_1'=4,'seq_2'=2] {'seq_2'}, use_global_device_ids=true, to_apply=%region_18.19 | all-reduce | flops 256 | bytes 2048 | tf_op jit(solution)/shard_map/psum | solution.py:19
  538.3 4.0 copy.81
  545.0 13.5 %fusion.33 = bf16[1,128,1536]{2,1,0:T(8,128)(2,1)} fusion(bf16[128,3,2048]{2,0,1:T(8,128)(2,1)S(1)} %reshape.756, bf16[1536,3,2048]{2,0,1:T(8,128)(2,1)} %all-gather.3.cloned.1.call-done), kind=kOutput, calls=%fused_computation.44 | convolution fusion | flops 2416115712 | bytes 20840448 | tf_op jit(solution)/shard_map/btch,dch->btd/dot_general | solution.py:143
  (188 shorter events, 197.4 us)
Async XLA Ops:
  8.0 216.0 %copy-start = (bf16[1,128,2048]{2,1,0:T(8,128)(2,1)S(1)}, bf16[1,128,2048]{2,1,0:T(8,128)(2,1)}, u32[]{:S(2)}) copy-start(bf16[1,128,2048]{2,1,0:T(8,128)(2,1)} %param.17) | copy-start | bytes 1572868
  8.0 195.7 %copy-start.15 = (bf16[1,128,1536]{2,1,0:T(8,128)(2,1)S(1)}, bf16[1,128,1536]{2,1,0:T(8,128)(2,1)}, u32[]{:S(2)}) copy-start(bf16[1,128,1536]{2,1,0:T(8,128)(2,1)} %param.11) | copy-start | bytes 1179652
  8.0 195.7 %all-gather.3.cloned.1.call-start = ((), (), s32[]{:S(2)}) async-start(), calls=%async_computation.5 | async-start | bytes 21233664 | tf_op jit(solution)/shard_map/all_gather | solution.py:104
  8.8 203.9 %copy-start.21 = (bf16[1,128,2048]{2,1,0:T(8,128)(2,1)S(1)}, bf16[1,128,2048]{2,1,0:T(8,128)(2,1)}, u32[]{:S(2)}) copy-start(bf16[1,128,2048]{2,1,0:T(8,128)(2,1)} %param.16) | copy-start | bytes 1572868
  215.5 40.0 %all-to-all-start = ((bf16[1,128,4,2048]{1,2,0,3:T(4,128)(2,1)}), bf16[1,128,4,2048]{1,2,0,3:T(4,128)(2,1)}, u32[]{:S(2)}, u32[]{:S(2)}) async-start(bf16[1,128,4,2048]{1,2,0,3:T(4,128)(2,1)} %copy.49), calls=%async_computation | async-start | bytes 4194304 | tf_op jit(solution)/shard_map/all_to_all | solution.py:109
  222.9 191.3 %all-gather.5.cloned.1.call-start = ((), (), s32[]{:S(2)}) async-start(), calls=%async_computation.6 | async-start | bytes 6684672 | tf_op jit(solution)/shard_map/all_gather | solution.py:149
  274.2 5.1 copy-start.23
  286.7 4.8 copy-start.3
  304.3 5.2 copy-start.3
  304.3 5.2 copy-start.20
  322.3 5.2 copy-start.3
  322.4 5.2 copy-start.20
  340.4 5.2 copy-start.3
  340.4 5.2 copy-start.20
  359.3 5.0 copy-start.6
  367.8 9.0 %copy-start.19 = (bf16[1,128,1536]{2,1,0:T(8,128)(2,1)S(1)}, bf16[1,128,1536]{2,1,0:T(8,128)(2,1)}, u32[]{:S(2)}) copy-start(bf16[1,128,1536]{2,1,0:T(8,128)(2,1)} %param.12) | copy-start | bytes 1179652
  369.6 14.8 %all-to-all-start.2 = ((bf16[1,128,3,128]{3,2,0,1:T(4,128)(2,1)}), bf16[1,128,3,128]{3,2,0,1:T(4,128)(2,1)S(1)}, u32[]{:S(2)}, u32[]{:S(2)}) async-start(bf16[1,128,3,128]{3,2,0,1:T(4,128)(2,1)} %copy.65), calls=%async_computation.2 | async-start | bytes 262144 | tf_op jit(solution)/shard_map/all_to_all | solution.py:137
  384.4 13.8 %copy-start.13 = (bf16[1,2176,1,128]{1,3,2,0:T(8,128)(2,1)S(1)}, bf16[1,2176,1,128]{1,3,2,0:T(8,128)(2,1)}, u32[]{:S(2)}) copy-start(bf16[1,2176,1,128]{1,3,2,0:T(8,128)(2,1)} %copy-done.12) | copy-start | bytes 1671172
  393.4 4.8 copy-start.9
  394.2 13.9 %all-to-all-start.3 = ((bf16[16,1,8,1536]{3,2,1,0:T(8,128)(2,1)}), bf16[16,1,8,1536]{3,2,1,0:T(8,128)(2,1)S(1)}, u32[]{:S(2)}, u32[]{:S(2)}) async-start(bf16[16,1,8,1536]{3,2,1,0:T(8,128)(2,1)} %broadcast_in_dim.17), calls=%async_computation.3 | async-start | bytes 786432 | tf_op jit(solution)/shard_map/all_to_all | solution.py:25
  408.8 129.6 %all-to-all-start.1 = ((bf16[1,2048,3,128]{3,2,0,1:T(4,128)(2,1)}), bf16[1,2048,3,128]{3,2,0,1:T(4,128)(2,1)}, u32[]{:S(2)}, u32[]{:S(2)}) async-start(bf16[1,2048,3,128]{3,2,0,1:T(4,128)(2,1)} %copy.63), calls=%async_computation.1 | async-start | bytes 4194304 | tf_op jit(solution)/shard_map/all_to_all | solution.py:136
  414.2 144.3 %reduce-scatter.2.cloned.1.call-start = ((), (), s32[]{:S(2)}) async-start(), calls=%async_computation.7 | async-start | bytes 1327104 | tf_op jit(solution)/shard_map/reduce_scatter | solution.py:165
  544.9 15.2 %copy-start.17 = (bf16[16,1,8,1536]{3,2,1,0:T(8,128)(2,1)S(1)}, bf16[16,1,8,1536]{3,2,1,0:T(8,128)(2,1)}, u32[]{:S(2)}) copy-start(bf16[16,1,8,1536]{3,2,1,0:T(8,128)(2,1)} %copy-done.16) | copy-start | bytes 1179652
  544.9 15.9 %copy-start.1 = (bf16[1,128,2048]{2,1,0:T(8,128)(2,1)S(1)}, bf16[1,128,2048]{2,1,0:T(8,128)(2,1)}, u32[]{:S(2)}) copy-start(bf16[1,128,2048]{2,1,0:T(8,128)(2,1)} %param.17) | copy-start | bytes 1572868
  (20 other events, 43.4 us)
Sparse Core Ops, SparseCore 0:
  10.5 193.1 all-gather.2
  504.9 33.6 reduce-scatter.1
Sparse Core Ops, SparseCore 1:
  226.2 74.2 all-gather.4
where the time goes:
time: 571 us; the launch traced here: 568 us
  waiting for transfers between devices  237 us (42%)
  matrix products  124 us (22%)
  other arithmetic  74.9 us (13%)
  local copies, waits for them, and re-layouts  58.3 us (10%)
  blocking collectives  33.6 us (6%)
  starting transfers between devices  24.2 us (4%)
  between operations  15.8 us (3%)
    all_gather x1, waiting for transfers between devices, local(): weights = lax.all_gather(w_qkv, FSDP, axis=0, tiled=True)  195 us
    add x16, other arithmetic, add_block(): return running + rounded.astype(jnp.float32)  50.8 us
    dot_general x16, matrix products, add_block(): jnp.einsum('btd,btch->dch', image_block, grad_block, preferred_element_ty...  36.6 us
    psum x5, blocking collectives, over_axes(): shard = lax.psum(shard, axis)  33.6 us
    all_to_all x1, waiting for transfers between devices, local(): lax.all_to_all(stacked, SEQ, split_axis=3, concat_axis=1, tiled=True)  29.6 us
    dot_general x4, matrix products, visit(): jnp.dot(attention.astype(jnp.bfloat16).T, incoming_piece, preferred_eleme...  20.2 us
    dot_general x1, matrix products, local(): jnp.einsum('btch,dch->btd', image_tokens, weights, preferred_element_type...  13.5 us
    unnamed x46, local copies, waits for them, and re-layouts  11.6 us
  transfers between devices with their start and end apart: 7, of which 4 were waited for; matrix products, arithmetic and copies ran while one was open for 40% of the time, Pallas kernels for 0%

commit v1 on v0

--- a/solution.py
+++ b/solution.py
@@ -101,7 +101,9 @@
     offset = own_index * own_width
     text_length = text_input.shape[1]
     image_rows_dev = image_input.shape[1]
-    weights = lax.all_gather(w_qkv, FSDP, axis=0, tiled=True)
+    weights = jnp.concatenate(
+        lax.all_to_all(jnp.stack([w_qkv] * lax.axis_size(FSDP)), FSDP, 0, 0), axis=0
+    )
     image_triple = jnp.einsum(
         "btd,dch->btch", image_input, weights, preferred_element_type=jnp.float32
     ).astype(jnp.bfloat16)

time: 571 us -> 602 us (1.054)
  blocking collectives: 33.6 us -> 247 us
  waiting for transfers between devices: 237 us -> 41.7 us
  local copies, waits for them, and re-layouts: 58.3 us -> 76 us
  matrix products: 124 us -> 117 us
    all_to_all x0 -> x1, blocking collectives: none -> 214 us  [local(): lax.all_to_all(jnp.stack([w_qkv] * lax.axis_size(FSDP)), FSDP, 0, 0)]
    all_gather x1 -> x0, waiting for transfers between devices: 195 us -> none  [local(): weights = lax.all_gather(w_qkv, FSDP, axis=0, tiled=True)]
    all_to_all x0 -> x1, local copies, waits for them, and re-layouts: none -> 9.8 us  [local(): lax.all_to_all(jnp.stack([w_qkv] * lax.axis_size(FSDP)), FSDP, 0, 0)]
    dot_general x1, matrix products: 8.98 us -> 2.62 us  [local(): jnp.einsum('btd,dch->btch', image_input, weights, preferred_element_type=...]
    unnamed x46 -> x48, local copies, waits for them, and re-layouts: 11.6 us -> 15.5 us
  transfers between devices with their start and end apart: 7 -> 6, of which waited for: 4 -> 3; matrix products, arithmetic and copies ran while one was open for 40% -> 37% of each run, Pallas kernels for 0% -> 0%
where the time goes in v1:
time: 602 us; the launch traced here: 600 us
  blocking collectives  247 us (41%)
  matrix products  117 us (19%)
  local copies, waits for them, and re-layouts  76 us (13%)
  other arithmetic  75.1 us (12%)
  waiting for transfers between devices  41.7 us (7%)
  starting transfers between devices  27 us (4%)
  between operations  14.4 us (2%)
    all_to_all x1, blocking collectives, local(): lax.all_to_all(jnp.stack([w_qkv] * lax.axis_size(FSDP)), FSDP, 0, 0)  214 us
    add x16, other arithmetic, add_block(): return running + rounded.astype(jnp.float32)  50.9 us
    dot_general x16, matrix products, add_block(): jnp.einsum('btd,btch->dch', image_block, grad_block, preferred_element_ty...  36.6 us
    psum x5, blocking collectives, over_axes(): shard = lax.psum(shard, axis)  33.4 us
    all_to_all x1, waiting for transfers between devices, local(): lax.all_to_all(stacked, SEQ, split_axis=3, concat_axis=1, tiled=True)  29.6 us
    dot_general x4, matrix products, visit(): jnp.dot(attention.astype(jnp.bfloat16).T, incoming_piece, preferred_eleme...  20.2 us
    unnamed x48, local copies, waits for them, and re-layouts  15.5 us
    dot_general x1, matrix products, local(): jnp.einsum('btch,dch->btd', image_tokens, weights, preferred_element_type...  13.5 us
  transfers between devices with their start and end apart: 6, of which 3 were waited for; matrix products, arithmetic and copies ran while one was open for 37% of the time, Pallas kernels for 0%

profile of v1, /device:TPU:1, one launch (start us, length us, event | category | flops | bytes accessed | tf_op | source)
XLA Modules:
  0.0 599.6 jit_solution(14147137257216403380)
XLA Ops:
  7.2 4.4 stack.32
  11.6 214.0 %all_to_all.58 = bf16[8,192,3,2048]{3,1,2,0:T(8,128)(2,1)} all-to-all(bf16[8,192,3,2048]{3,1,2,0:T(8,128)(2,1)S(1)} %stack.32), channel_id=1, replica_groups=mesh['fsdp_0'=2,'fsdp_1'=4,'seq_0'=2,'seq_1'=4,'seq_2'=2] {'fsdp_0','fsd..., dimensions={0} | all-to-all | bytes 37748736 | tf_op jit(solution)/shard_map/all_to_all | solution.py:105
  225.6 9.8 %copy.49 = bf16[8,192,3,2048]{3,1,0,2:T(8,128)(2,1)S(1)} copy(bf16[8,192,3,2048]{3,1,2,0:T(8,128)(2,1)} %all_to_all.58) | data formatting | bytes 37748736 | tf_op jit(solution)/shard_map/all_to_all | solution.py:105
  244.6 9.9 %all-to-all-start.1 = ((bf16[1,128,4,2048]{1,2,0,3:T(4,128)(2,1)}), bf16[1,128,4,2048]{1,2,0,3:T(4,128)(2,1)}, u32[]{:S(2)}, u32[]{:S(2)}) async-start(bf16[1,128,4,2048]{1,2,0,3:T(4,128)(2,1)} %copy.50), calls=%async_computation.1 | async-start | bytes 4194304 | tf_op jit(solution)/shard_map/all_to_all | solution.py:111
  257.5 29.6 %all-to-all-done.1 = bf16[1,128,4,2048]{1,2,0,3:T(4,128)(2,1)} async-done(((bf16[1,128,4,2048]{1,2,0,3:T(4,128)(2,1)}), bf16[1,128,4,2048]{1,2,0,3:T(4,128)(2,1)}, u32[]{:S(2)}, u32[]{:S(2)}) %all-to-all-start.1) | async-done | bytes 2097184 | tf_op jit(solution)/shard_map/all_to_all | solution.py:111
  287.1 4.3 copy.81
  291.4 4.2 all_to_all.45
  313.3 71.6 %while.29 = (s32[]{:T(128)}, f32[1,1,2176,128]{3,2,1,0:T(8,128)S(1)}, f32[1,1,2176,128]{3,2,1,0:T(8,128)}, f32[4,1,1,544,128]{4,3,2,1,0:T(8,128)}, bf16[4,1,1,54...) while((s32[]{:T(128)}, ...), condition=%wide.region_6.7_spmd.clone, body=%wide.region_2.6_spmd.clone.sunk | while | flops 1535592832 | bytes 89573472 | solution.py:82
  318.3 4.8 fusion.106
  335.9 5.1 fusion.106
  353.9 5.1 fusion.106
  371.9 5.1 fusion.106
  401.1 7.6 %all-to-all-start.3 = ((bf16[1,128,3,128]{3,2,0,1:T(4,128)(2,1)}), bf16[1,128,3,128]{3,2,0,1:T(4,128)(2,1)S(1)}, u32[]{:S(2)}, u32[]{:S(2)}) async-start(bf16[1,128,3,128]{3,2,0,1:T(4,128)(2,1)} %copy.66), calls=%async_computation.3 | async-start | bytes 262144 | tf_op jit(solution)/shard_map/all_to_all | solution.py:139
  411.1 5.1 all-to-all-done.3
  416.2 9.0 %fusion.34 = bf16[8,1536]{1,0:T(8,128)(2,1)S(1)} fusion(bf16[1536,3,2048]{2,0,1:T(8,128)(2,1)} %bitcast.221, bf16[1,128,3,128]{3,2,0,1:T(4,128)(2,1)S(1)} %all-to-all-done.3), kind=kOutput, calls=%fused_computation.46 | convolution fusion | flops 151007232 | bytes 18997248 | tf_op jit(solution)/shard_map/btch,dch->btd/dot_general | solution.py:141
  433.0 6.9 %all-to-all-done.4 = bf16[16,1,8,1536]{3,2,1,0:T(8,128)(2,1)S(1)} async-done(((bf16[16,1,8,1536]{3,2,1,0:T(8,128)(2,1)}), bf16[16,1,8,1536]{3,2,1,0:T(8,128)(2,1)S(1)}, u32[]{:S(2)}, u32[]{:S(2)}) %all-to-all-start.4) | async-done | bytes 393248 | tf_op jit(solution)/shard_map/all_to_all | solution.py:25
  440.6 5.4 all-to-all-start.2
  446.1 87.8 %while.30 = (s32[]{:T(128)}, f32[1536,3,128]{2,0,1:T(8,128)}, bf16[1,2048,1536]{1,2,0:T(8,128)(2,1)}, bf16[1,2048,3,128]{1,3,2,0:T(8,128)(2,1)S(1)}, s32[]{:T(12...) while((s32[]{:T(128)}, f32[1536,3,128]{2,0,1:T(8,128)}, ...), condition=%wide.region_10.11_spmd.clone, body=%wide.region_9.10_spmd.clone.sunk | while | flops 154533888 | bytes 9930411 | solution.py:166
  540.6 6.1 %psum.36 = f32[2,128]{1,0:T(2,128)S(1)} all-reduce(f32[2,128]{1,0:T(2,128)S(1)} %psum.35), channel_id=1, replica_groups=mesh['fsdp_0'=2,'fsdp_1'=4,'seq_0'=2,'seq_1'=4,'seq_2'=2] {'fsdp_1'}, use_global_device_ids=true, to_apply=%region_15.16 | all-reduce | flops 256 | bytes 2048 | tf_op jit(solution)/shard_map/psum | solution.py:19
  546.7 5.7 psum.37
  552.4 9.0 %psum.38 = f32[2,128]{1,0:T(2,128)S(1)} all-reduce(f32[2,128]{1,0:T(2,128)S(1)} %psum.37), channel_id=1, replica_groups=mesh['fsdp_0'=2,'fsdp_1'=4,'seq_0'=2,'seq_1'=4,'seq_2'=2] {'seq_1'}, use_global_device_ids=true, to_apply=%region_17.18 | all-reduce | flops 256 | bytes 2048 | tf_op jit(solution)/shard_map/psum | solution.py:19
  561.4 8.8 %psum.39 = f32[2,128]{1,0:T(2,128)} all-reduce(f32[2,128]{1,0:T(2,128)S(1)} %psum.38), channel_id=1, replica_groups=mesh['fsdp_0'=2,'fsdp_1'=4,'seq_0'=2,'seq_1'=4,'seq_2'=2] {'seq_2'}, use_global_device_ids=true, to_apply=%region_18.19 | all-reduce | flops 256 | bytes 2048 | tf_op jit(solution)/shard_map/psum | solution.py:19
  570.2 4.0 copy.82
  576.8 13.5 %fusion.33 = bf16[1,128,1536]{2,1,0:T(8,128)(2,1)} fusion(bf16[128,3,2048]{2,0,1:T(8,128)(2,1)S(1)} %reshape.762, bf16[1536,3,2048]{2,0,1:T(8,128)(2,1)} %bitcast.222), kind=kOutput, calls=%fused_computation.44 | convolution fusion | flops 2416115712 | bytes 20840448 | tf_op jit(solution)/shard_map/btch,dch->btd/dot_general | solution.py:145
  (190 shorter events, 207.0 us)
Async XLA Ops:
  7.2 248.4 %copy-start = (bf16[1,128,2048]{2,1,0:T(8,128)(2,1)S(1)}, bf16[1,128,2048]{2,1,0:T(8,128)(2,1)}, u32[]{:S(2)}) copy-start(bf16[1,128,2048]{2,1,0:T(8,128)(2,1)} %param.17) | copy-start | bytes 1572868
  225.6 9.8 %copy-start.16 = (bf16[1,128,1536]{2,1,0:T(8,128)(2,1)S(1)}, bf16[1,128,1536]{2,1,0:T(8,128)(2,1)}, u32[]{:S(2)}) copy-start(bf16[1,128,1536]{2,1,0:T(8,128)(2,1)} %param.11) | copy-start | bytes 1179652
  235.4 6.4 %copy-start.4 = (bf16[8,192,3,2048]{3,1,0,2:T(8,128)(2,1)}, bf16[8,192,3,2048]{3,1,0,2:T(8,128)(2,1)S(1)}, u32[]{:S(2)}) copy-start(bf16[8,192,3,2048]{3,1,0,2:T(8,128)(2,1)S(1)} %copy.49) | copy-start | bytes 56623108
  235.4 6.4 %copy-start.22 = (bf16[1,128,2048]{2,1,0:T(8,128)(2,1)S(1)}, bf16[1,128,2048]{2,1,0:T(8,128)(2,1)}, u32[]{:S(2)}) copy-start(bf16[1,128,2048]{2,1,0:T(8,128)(2,1)} %param.16) | copy-start | bytes 1572868
  244.6 42.6 %all-to-all-start.1 = ((bf16[1,128,4,2048]{1,2,0,3:T(4,128)(2,1)}), bf16[1,128,4,2048]{1,2,0,3:T(4,128)(2,1)}, u32[]{:S(2)}, u32[]{:S(2)}) async-start(bf16[1,128,4,2048]{1,2,0,3:T(4,128)(2,1)} %copy.50), calls=%async_computation.1 | async-start | bytes 4194304 | tf_op jit(solution)/shard_map/all_to_all | solution.py:111
  254.5 191.6 %all-gather.2.cloned.1.call-start = ((), (), s32[]{:S(2)}) async-start(), calls=%async_computation.6 | async-start | bytes 6684672 | tf_op jit(solution)/shard_map/all_gather | solution.py:151
  305.7 5.1 copy-start.24
  318.3 4.8 copy-start.3
  335.9 5.2 copy-start.3
  335.9 5.2 copy-start.21
  353.9 5.2 copy-start.3
  353.9 5.2 copy-start.21
  371.9 5.2 copy-start.3
  371.9 5.2 copy-start.21
  390.8 5.0 copy-start.7
  399.3 9.4 %copy-start.20 = (bf16[1,128,1536]{2,1,0:T(8,128)(2,1)S(1)}, bf16[1,128,1536]{2,1,0:T(8,128)(2,1)}, u32[]{:S(2)}) copy-start(bf16[1,128,1536]{2,1,0:T(8,128)(2,1)} %param.12) | copy-start | bytes 1179652
  401.1 15.2 %all-to-all-start.3 = ((bf16[1,128,3,128]{3,2,0,1:T(4,128)(2,1)}), bf16[1,128,3,128]{3,2,0,1:T(4,128)(2,1)S(1)}, u32[]{:S(2)}, u32[]{:S(2)}) async-start(bf16[1,128,3,128]{3,2,0,1:T(4,128)(2,1)} %copy.66), calls=%async_computation.3 | async-start | bytes 262144 | tf_op jit(solution)/shard_map/all_to_all | solution.py:139
  416.2 13.8 %copy-start.14 = (bf16[1,2176,1,128]{1,3,2,0:T(8,128)(2,1)S(1)}, bf16[1,2176,1,128]{1,3,2,0:T(8,128)(2,1)}, u32[]{:S(2)}) copy-start(bf16[1,2176,1,128]{1,3,2,0:T(8,128)(2,1)} %copy-done.13) | copy-start | bytes 1671172
  425.2 4.8 copy-start.10
  426.0 13.9 %all-to-all-start.4 = ((bf16[16,1,8,1536]{3,2,1,0:T(8,128)(2,1)}), bf16[16,1,8,1536]{3,2,1,0:T(8,128)(2,1)S(1)}, u32[]{:S(2)}, u32[]{:S(2)}) async-start(bf16[16,1,8,1536]{3,2,1,0:T(8,128)(2,1)} %broadcast_in_dim.17), calls=%async_computation.4 | async-start | bytes 786432 | tf_op jit(solution)/shard_map/all_to_all | solution.py:25
  440.6 129.6 %all-to-all-start.2 = ((bf16[1,2048,3,128]{3,2,0,1:T(4,128)(2,1)}), bf16[1,2048,3,128]{3,2,0,1:T(4,128)(2,1)}, u32[]{:S(2)}, u32[]{:S(2)}) async-start(bf16[1,2048,3,128]{3,2,0,1:T(4,128)(2,1)} %copy.64), calls=%async_computation.2 | async-start | bytes 4194304 | tf_op jit(solution)/shard_map/all_to_all | solution.py:138
  446.0 144.3 %reduce-scatter.2.cloned.1.call-start = ((), (), s32[]{:S(2)}) async-start(), calls=%async_computation.7 | async-start | bytes 1327104 | tf_op jit(solution)/shard_map/reduce_scatter | solution.py:167
  576.8 15.2 %copy-start.18 = (bf16[16,1,8,1536]{3,2,1,0:T(8,128)(2,1)S(1)}, bf16[16,1,8,1536]{3,2,1,0:T(8,128)(2,1)}, u32[]{:S(2)}) copy-start(bf16[16,1,8,1536]{3,2,1,0:T(8,128)(2,1)} %copy-done.17) | copy-start | bytes 1179652
  576.8 15.9 %copy-start.1 = (bf16[1,128,2048]{2,1,0:T(8,128)(2,1)S(1)}, bf16[1,128,2048]{2,1,0:T(8,128)(2,1)}, u32[]{:S(2)}) copy-start(bf16[1,128,2048]{2,1,0:T(8,128)(2,1)} %param.17) | copy-start | bytes 1572868
  (20 other events, 43.2 us)
Sparse Core Ops, SparseCore 0:
  258.2 74.0 all-gather.1
  536.9 33.4 reduce-scatter.1
